TPU v7x, 256 devices: a whole 4x4x8 slice. The times are simulated.
256 devices in a mesh: seq: 32 (over z, x), tp: 8 (over y, core).
Axes of the slice: x: 4, y: 4, z: 8, core: 2. Of those that a mesh axis runs over, the one named last changes fastest.
Arguments:
- queries: bfloat16 [8192, 8192], P('seq', 'tp'), may hold values from -120 to 120
- keys: bfloat16 [8192, 1024], P('seq', 'tp'), may hold values from -5 to 5
- values: bfloat16 [8192, 1024], P('seq', 'tp'), may hold values from -6 to 6
- w_query: bfloat16 [8192, 8192], P('seq', 'tp'), may hold values from -0.0625 to 0.0625
- key_weight: bfloat16 [8192, 1024], P('seq'), may hold values from -0.0625 to 0.0625
Outputs:
- attended: bfloat16 [8192, 8192], P('seq', 'tp')
- head_logit_maxima: float32 [64], P('tp')
- w_query_clipped: bfloat16 [8192, 8192], P('seq', 'tp')
- clipped_key_weight: bfloat16 [8192, 1024], P('seq')
All inputs are finite; a program needn't handle non-finite values.
Results may differ from a plain program's by a relative error of at most 0.004.
Values may be sent and summed in bfloat16 or wider, within the bound.
A program may use at most 64 MiB of HBM per device.

v0:
```python
from functools import partial
import math

import jax
import jax.numpy as jnp
from jax import lax
from jax.sharding import PartitionSpec as P

HEAD_SIZE = 128


clip_threshold = 10.0


def in_one_piece(arrays, axis, dim, along):
    both = jnp.concatenate(arrays, axis=along)
    filled, at, finished = (lax.all_gather(both, axis, axis=dim, tiled=True), 0, [])
    for a in arrays:
        finished.append(lax.slice_in_dim(filled, at, at + a.shape[along], axis=along))
        at += a.shape[along]
    return tuple(finished)


def sent_to_all(value, axis):
    count = lax.axis_size(axis)
    return lax.all_to_all(
        jnp.broadcast_to(value[None], (count, *value.shape)), axis, 0, 0, tiled=True
    )


def over_copies(value, axis):
    everything = sent_to_all(value, axis)
    return jnp.max(everything, axis=0)


def in_order(pieces, dim):
    lengths = list(pieces.shape[1:])
    lengths[dim] *= pieces.shape[0]
    return jnp.moveaxis(pieces, 0, dim).reshape(lengths)


def collect(value, axis, dim):
    pieces = sent_to_all(value, axis)
    return in_order(pieces, dim)


def attend_block(state, query_rows, positions, key_block, value_block, block_start, kv_heads):
    row_max, row_sum, weighted, head_max = state
    piece_rows = key_block.shape[0]
    half_rows = query_rows.shape[0]
    query_heads_view = query_rows.reshape(half_rows, kv_heads, -1, HEAD_SIZE)
    key_heads_view = key_block.reshape(piece_rows, kv_heads, HEAD_SIZE)
    value_heads_view = value_block.reshape(piece_rows, kv_heads, HEAD_SIZE)
    scores = jnp.einsum(
        "rkgd,nkd->rkgn", query_heads_view, key_heads_view, preferred_element_type=jnp.float32
    ) * HEAD_SIZE ** (-0.5)
    visible = (
        positions[:, None] >= block_start + jnp.arange(piece_rows, dtype=jnp.int32)[None, :]
    )[:, None, None, :]
    masked = jnp.where(visible, scores, jnp.float32(-1e30))
    block_row_max = masked.max(-1)
    new_max = jnp.maximum(row_max, block_row_max)
    expo = jnp.where(visible, jnp.exp(masked - new_max[..., None]), jnp.float32(0.0))
    carry_scale = jnp.exp(row_max - new_max)
    row_sum = row_sum * carry_scale + expo.sum(-1)
    product = jnp.einsum(
        "rkgn,nkd->rkgd",
        expo.astype(jnp.bfloat16),
        value_heads_view,
        preferred_element_type=jnp.float32,
    )
    weighted = weighted * carry_scale[..., None] + product
    head_max = jnp.maximum(head_max, block_row_max.max(0))
    return (new_max, row_sum, weighted, head_max)


def keep_state(state):
    return state


def shards(queries, keys, values, w_query, key_weight):
    tok_rows = queries.shape[0]
    half_rows = tok_rows // 2
    heads = queries.shape[1] // HEAD_SIZE
    kv_heads = keys.shape[1] // HEAD_SIZE
    group_size = heads // kv_heads
    seq_index = lax.axis_index("seq")
    all_rows = jnp.arange(tok_rows, dtype=jnp.int32)
    positions = seq_index * tok_rows + all_rows
    lower_queries = queries[:half_rows]
    upper_queries = queries[half_rows:]
    lower_positions = positions[:half_rows]
    upper_positions = positions[half_rows:]

    def fresh_state():
        return (
            jnp.full((half_rows, kv_heads, group_size), -1e30, jnp.float32),
            jnp.zeros((half_rows, kv_heads, group_size), jnp.float32),
            jnp.zeros((half_rows, kv_heads, group_size, HEAD_SIZE), jnp.float32),
            jnp.full((kv_heads, group_size), -1e30, jnp.float32),
        )

    halves = ((lower_queries, lower_positions), (upper_queries, upper_positions))
    key_piece, value_piece = in_one_piece((keys, values), "seq", 0, 1)
    piece_rows = key_piece.shape[0]
    block_rows = math.gcd(piece_rows, 2048)

    def one_block(block_index, states):
        block_start = block_index * block_rows
        key_block = lax.dynamic_slice_in_dim(key_piece, block_index * block_rows, block_rows, 0)
        value_block = lax.dynamic_slice_in_dim(value_piece, block_index * block_rows, block_rows, 0)
        updated = []
        for state, (query_rows, row_positions) in zip(states, halves):
            worker = partial(
                attend_block,
                query_rows=query_rows,
                positions=row_positions,
                key_block=key_block,
                value_block=value_block,
                block_start=block_start,
                kv_heads=kv_heads,
            )
            updated.append(lax.cond(block_start <= row_positions.max(), worker, keep_state, state))
        return tuple(updated)

    lower_state, upper_state = lax.fori_loop(
        0, piece_rows // block_rows, one_block, (fresh_state(), fresh_state())
    )

    def finish(state):
        return (
            (state[2] / state[1][..., None])
            .reshape(half_rows, heads * HEAD_SIZE)
            .astype(jnp.bfloat16)
        )

    attended = jnp.concatenate([finish(lower_state), finish(upper_state)], axis=0)
    local_max = jnp.maximum(lower_state[3], upper_state[3]).reshape(heads)
    head_max = over_copies(local_max, "seq")
    group_local = clip_threshold / jnp.maximum(
        head_max.reshape(kv_heads, group_size).max(1), clip_threshold
    )
    factors_all = collect(group_local, "tp", 0)
    gamma = clip_threshold / jnp.maximum(head_max, clip_threshold)
    query_factor = gamma / jnp.sqrt(jnp.repeat(group_local, group_size))
    weight_rows = w_query.shape[0]
    w_query_clipped = (
        (
            w_query.astype(jnp.float32).reshape(weight_rows, heads, HEAD_SIZE)
            * query_factor[None, :, None]
        )
        .reshape(weight_rows, heads * HEAD_SIZE)
        .astype(jnp.bfloat16)
    )
    all_kv = key_weight.shape[1] // HEAD_SIZE
    clipped_key_weight = (
        (
            key_weight.astype(jnp.float32).reshape(weight_rows, all_kv, HEAD_SIZE)
            * jnp.sqrt(factors_all)[None, :, None]
        )
        .reshape(weight_rows, all_kv * HEAD_SIZE)
        .astype(jnp.bfloat16)
    )
    return (attended, head_max, w_query_clipped, clipped_key_weight)


def solution(mesh):
    in_specs = (P("seq", "tp"), P("seq", "tp"), P("seq", "tp"), P("seq", "tp"), P("seq", None))
    out_specs = (P("seq", "tp"), P("tp"), P("seq", "tp"), P("seq", None))
    return jax.shard_map(shards, mesh=mesh, in_specs=in_specs, out_specs=out_specs, check_vma=False)
```

profile of v0, /device:TPU:32, one launch (start us, length us, event | category | flops | bytes accessed | tf_op | source)
XLA Modules:
  0.0 206.4 jit_solution(11001129317073461309)
XLA Ops:
  7.2 0.0 all-gather.2.cloned.1.call-start
  7.2 1.5 pad_maximum_fusion.1
  8.8 0.0 all-gather.2.cloned.1.call-update
  8.8 0.6 slice_reduce_fusion
  9.4 1.1 fusion.48
  10.5 84.7 %all-gather.2.cloned.1.call-done = bf16[8192,256]{1,0:T(8,128)(2,1)} async-done(((bf16[256,256]{1,0:T(8,128)(2,1)}), bf16[8192,256]{1,0:T(8,128)(2,1)}) %all-gather.2.cloned.1.call-update) | async-done | bytes 4194320 | tf_op jit(solution)/shard_map/all_gather | solution.py:17
  95.2 4.5 %fusion.47 = (bf16[8192,128]{1,0:T(8,128)(2,1)}, bf16[8192,128]{1,0:T(8,128)(2,1)}) fusion(bf16[8192,256]{1,0:T(8,128)(2,1)} %all-gather.2.cloned.1.call-done), kind=kLoop, calls=%fused_computation.71 | loop fusion | bytes 8388608 | tf_op jit(solution)/shard_map/slice | solution.py:19
  99.8 0.0 copy-start
  99.8 25.8 %while.28 = (s32[]{:T(128)}, f32[128,1,8]{0,2,1:T(8,128)S(1)}, f32[128,1,8]{0,2,1:T(8,128)S(1)}, f32[128,1,8,128]{3,0,2,1:T(8,128)S(1)}, f32[1,8]{1,0:T(1,128)S(...) while((s32[]{:T(128)}, f32[128,1,8]{0,2,1:T(8,128)S(1)}, ...), condition=%wide.region_13.14_spmd, body=%wide.region_2.13_spmd.sunk | while | flops 2207262720 | bytes 59410224 | solution.py:126
  101.2 1.3 constant_dynamic-slice_fusion.3
  102.5 7.6 %conditional.4 = ((f32[128,1,8]{0,2,1:T(8,128)S(1)}, f32[128,1,8]{0,2,1:T(8,128)S(1)}, f32[128,1,8,128]{3,0,2,1:T(8,128)S(1)}, f32[1,8]{1,0:T(1,128)S(1)})) conditional(s32[]{:T(128)} %convert_element_type.78, (f32[128,1,8]{0,2,1:T(8,128)S(1)}, f32[128,1,8]{0,2,1:T(8,128)S(1)}, f32[128,1,8,128]{3,0,2,1:T(8,128)S(1)}, f32[1,8]{1,0:T(1,128)S(1)}) %tuple.70, ...), branch_computations={%region_3.3_spmd, %region_4.7_spmd} | conditional | flops 1103631360 | bytes 28656300 | solution.py:123
  102.5 0.3 broadcast_compare_fusion
  102.9 1.4 fusion.3
  104.2 2.6 %fusion.11 = f32[128,1,8,128]{3,0,2,1:T(8,128)S(1)} fusion(f32[2048,128,8]{1,0,2:T(8,128)S(1)} %get-tuple-element.477, f32[128,8]{0,1:T(8,128)S(1)} %bitcast.142, pred[128,2048]{0,1:T(8,128)(4,1)S(1)} %broadcast_compare_fusion, bf16[2048,128]{1,0:T(8,128)(2,1)S(1)} %get-tuple-element.377, f32[128,1,8,128]{3,0,2,1:T(8,128)S(1)} %get-tuple-element.376, ...), kind=kOutput, calls=%fused_computation.10 | convolution fusion | flops 547618816 | bytes 10231808 | tf_op jit(solution)/shard_map/while/body/eval_jaxpr/cond/branch_1_fun/rkgn,nkd->rkgd/dot_general | solution.py:66
  106.9 3.2 %fusion.2 = (f32[8]{0:T(128)S(1)}, f32[128,8]{0,1:T(8,128)S(1)}) fusion(f32[2048,128,8]{1,0,2:T(8,128)S(1)} %get-tuple-element.477, pred[128,2048]{0,1:T(8,128)(4,1)S(1)} %broadcast_compare_fusion, f32[128,8]{0,1:T(8,128)S(1)} %bitcast.143), kind=kLoop, calls=%fused_computation.4 | loop fusion | flops 12581880 | bytes 8658976 | tf_op jit(solution)/shard_map/while/body/eval_jaxpr/cond/branch_1_fun/reduce_max | solution.py:73
  110.1 7.6 %conditional.5 = ((f32[128,1,8]{0,2,1:T(8,128)S(1)}, f32[128,1,8]{0,2,1:T(8,128)S(1)}, f32[128,1,8,128]{3,0,2,1:T(8,128)S(1)}, f32[1,8]{1,0:T(1,128)S(1)})) conditional(s32[]{:T(128)} %convert_element_type.79, (f32[128,1,8]{0,2,1:T(8,128)S(1)}, f32[128,1,8]{0,2,1:T(8,128)S(1)}, f32[128,1,8,128]{3,0,2,1:T(8,128)S(1)}, ...), branch_computations={%region_8.8_spmd, %region_9.12_spmd} | conditional | flops 1103631360 | bytes 28656300 | solution.py:123
  110.1 0.3 broadcast_compare_fusion.1
  110.4 1.4 fusion.26
  111.8 2.6 %fusion.34 = f32[128,1,8,128]{3,0,2,1:T(8,128)S(1)} fusion(f32[2048,128,8]{1,0,2:T(8,128)S(1)} %get-tuple-element.479, f32[128,8]{0,1:T(8,128)S(1)} %bitcast.144, pred[128,2048]{0,1:T(8,128)(4,1)S(1)} %broadcast_compare_fusion.1, bf16[2048,128]{1,0:T(8,128)(2,1)S(1)} %get-tuple-element.386, f32[128,1,8,128]{3,0,2,1:T(8,128)S(1)} %get-tuple-element.385, ...), kind=kOutput, calls=%fused_computation.36 | convolution fusion | flops 547618816 | bytes 10231808 | tf_op jit(solution)/shard_map/while/body/eval_jaxpr/cond/branch_1_fun/rkgn,nkd->rkgd/dot_general | solution.py:66
  114.4 3.2 %fusion.25 = (f32[8]{0:T(128)S(1)}, f32[128,8]{0,1:T(8,128)S(1)}) fusion(f32[2048,128,8]{1,0,2:T(8,128)S(1)} %get-tuple-element.479, pred[128,2048]{0,1:T(8,128)(4,1)S(1)} %broadcast_compare_fusion.1, f32[128,8]{0,1:T(8,128)S(1)} %bitcast.145), kind=kLoop, calls=%fused_computation.30 | loop fusion | flops 12581880 | bytes 8658976 | tf_op jit(solution)/shard_map/while/body/eval_jaxpr/cond/branch_1_fun/reduce_max | solution.py:73
  119.0 1.3 constant_dynamic-slice_fusion.3
  121.6 1.3 constant_dynamic-slice_fusion.3
  124.3 1.3 constant_dynamic-slice_fusion.3
  125.6 0.3 divide_convert_fusion
  126.0 0.2 copy.38
  126.2 0.6 broadcast_in_dim.58
  126.8 50.5 %all-to-all-start = ((f32[32,1,8]{2,1,0:T(1,128)}), f32[32,1,8]{2,1,0:T(1,128)S(1)}, u32[]{:S(2)}, u32[]{:S(2)}) async-start(f32[32,1,8]{2,1,0:T(1,128)} %broadcast_in_dim.58), calls=%async_computation | async-start | bytes 32768 | tf_op jit(solution)/shard_map/all_to_all | solution.py:26
  177.3 0.2 copy.37
  177.5 0.8 pad_maximum_fusion
  178.4 7.4 %all-to-all-done = f32[32,1,8]{2,1,0:T(1,128)S(1)} async-done(((f32[32,1,8]{2,1,0:T(1,128)}), f32[32,1,8]{2,1,0:T(1,128)S(1)}, u32[]{:S(2)}, u32[]{:S(2)}) %all-to-all-start) | async-done | bytes 1056 | tf_op jit(solution)/shard_map/all_to_all | solution.py:26
  185.8 0.6 fusion.46
  186.4 0.0 copy-start.1
  187.2 0.1 broadcast_bitcast_fusion.1
  187.3 0.6 broadcast_in_dim.59
  187.9 4.3 %all-to-all-start.1 = ((f32[8,1,1]{2,1,0:T(1,128)}), f32[8,1,1]{2,1,0:T(1,128)S(1)}, u32[]{:S(2)}, u32[]{:S(2)}) async-start(f32[8,1,1]{2,1,0:T(1,128)} %broadcast_in_dim.59), calls=%async_computation.1 | async-start | bytes 8192 | tf_op jit(solution)/shard_map/all_to_all | solution.py:26
  192.2 0.0 copy-done
  192.2 0.9 multiply_convert_fusion.1
  193.1 4.3 %all-to-all-done.1 = f32[8,1,1]{2,1,0:T(1,128)S(1)} async-done(((f32[8,1,1]{2,1,0:T(1,128)}), f32[8,1,1]{2,1,0:T(1,128)S(1)}, u32[]{:S(2)}, u32[]{:S(2)}) %all-to-all-start.1) | async-done | bytes 64 | tf_op jit(solution)/shard_map/all_to_all | solution.py:26
  197.4 0.2 sqrt_reduce_fusion
  197.5 0.1 broadcast_bitcast_fusion
  197.6 1.9 multiply_convert_fusion
  199.5 0.0 copy-done.1
  (29 shorter events, 0.4 us)
Async XLA Ops:
  7.2 88.1 %all-gather.2.cloned.1.call-start = ((), (), s32[]{:S(2)}) async-start(), calls=%async_computation.2 | async-start | bytes 4325376 | tf_op jit(solution)/shard_map/all_gather | solution.py:17
  99.8 92.3 %copy-start = (bf16[256,1024]{1,0:T(8,128)(2,1)S(1)}, bf16[256,1024]{1,0:T(8,128)(2,1)}, u32[]{:S(2)}) copy-start(bf16[256,1024]{1,0:T(8,128)(2,1)} %param.14) | copy-start | bytes 1572868
  126.8 59.0 %all-to-all-start = ((f32[32,1,8]{2,1,0:T(1,128)}), f32[32,1,8]{2,1,0:T(1,128)S(1)}, u32[]{:S(2)}, u32[]{:S(2)}) async-start(f32[32,1,8]{2,1,0:T(1,128)} %broadcast_in_dim.58), calls=%async_computation | async-start | bytes 32768 | tf_op jit(solution)/shard_map/all_to_all | solution.py:26
  186.4 13.1 %copy-start.1 = (f32[8]{0:T(128)}, f32[8]{0:T(128)S(1)}, u32[]{:S(2)}) copy-start(f32[8]{0:T(128)S(1)} %get-tuple-element.435) | copy-start | bytes 100
  187.9 9.5 %all-to-all-start.1 = ((f32[8,1,1]{2,1,0:T(1,128)}), f32[8,1,1]{2,1,0:T(1,128)S(1)}, u32[]{:S(2)}, u32[]{:S(2)}) async-start(f32[8,1,1]{2,1,0:T(1,128)} %broadcast_in_dim.59), calls=%async_computation.1 | async-start | bytes 8192 | tf_op jit(solution)/shard_map/all_to_all | solution.py:26
Sparse Core Ops, SparseCore 0:
  11.1 84.0 all-gather.1
where the time goes:
time: 209 us; the launch traced here: 206 us
  waiting for transfers between devices  96.5 us (46%)
  starting transfers between devices  54.8 us (26%)
  between operations  14.9 us (7%)
  other arithmetic  13.9 us (7%)
  local copies, waits for them, and re-layouts  12.7 us (6%)
  matrix products  7.96 us (4%)
  loops' own time  5.66 us (3%)
    all_gather x1, waiting for transfers between devices, in_one_piece(): lax.all_gather(both, axis, axis=dim, tiled=True)  84.7 us
    all_to_all x2, starting transfers between devices, sent_to_all(): lax.all_to_all(jnp.broadcast_to(value[None], (count, *value.shape)), axis...  54.8 us
    all_to_all x2, waiting for transfers between devices, sent_to_all(): lax.all_to_all(jnp.broadcast_to(value[None], (count, *value.shape)), axis...  11.7 us
    reduce_max x2, other arithmetic, attend_block(): head_max = jnp.maximum(head_max, block_row_max.max(0))  6.31 us
    another operation x1, loops' own time, shards(): lax.fori_loop(0, piece_rows // block_rows, one_block, (fresh_state(), fre...  5.43 us
    dot_general x2, matrix products, attend_block(): jnp.einsum('rkgn,nkd->rkgd', expo.astype(jnp.bfloat16), value_heads_view,...  5.25 us
    dynamic_slice x4, local copies, waits for them, and re-layouts, one_block(): lax.dynamic_slice_in_dim(value_piece, block_index * block_rows, block_row...  5.1 us
    slice x1, local copies, waits for them, and re-layouts, in_one_piece(): lax.slice_in_dim(filled, at, at + a.shape[along], axis=along)  4.46 us
  transfers between devices with their start and end apart: 3, of which 3 were waited for; matrix products, arithmetic and copies ran while one was open for 2% of the time, Pallas kernels for 0%

commit v1 on v0

v1 whole, which is shorter than its diff:
```python
import math

import jax
import jax.numpy as jnp
from jax import lax
from jax.experimental import pallas as pl
from jax.experimental.pallas import tpu as pltpu
from jax.sharding import PartitionSpec as P

HEAD = 128
ROWS = 256
NZ, NX = 8, 4
TAU = 10.0
NEG = -1e30
LOG2_SCALE = math.log2(math.e) / math.sqrt(128.0)
MESH = pl.DeviceIdType.MESH


def attention_kernel(q_hbm, k_hbm, v_hbm, o_hbm, hm_ref,
                     qv, kv, tr, qin, qhl, acc, mrow, res,
                     ld_sem, kv_sem, tr_sem, q_sem, o_sem,
                     zs_sem, xs_sem, ds_sem, qs_sem, os_sem):
    s = lax.axis_index("seq")
    t = lax.axis_index("tp")
    z = s // NX
    x = lax.rem(s, NX)
    c = lax.rem(t, 2)
    ch = z // (NZ // 2)
    driver = c == ch
    foreign = c != ch
    r = z + c * (NZ - 1 - 2 * z)
    rh = z + ch * (NZ - 1 - 2 * z)
    sib = t + 1 - 2 * c
    part = (NZ - 1 - z) * NX + (NX - 1 - x)
    xr = z * NX + lax.rem(x + 1, NX)
    xl = z * NX + lax.rem(x + NX - 1, NX)
    zu_z = lax.rem(z + NZ + 1 - 2 * c, NZ)
    zd_z = lax.rem(z + NZ - 1 + 2 * c, NZ)
    zu = zu_z * NX + x
    zd = zd_z * NX + x
    pu = lax.rem(r + 2, NZ)
    pd = lax.rem(NZ + 5 - r, NZ)

    own_k = pltpu.make_async_copy(k_hbm, kv.at[r, x, 0], ld_sem.at[0])
    own_v = pltpu.make_async_copy(v_hbm, kv.at[r, x, 1], ld_sem.at[1])
    tr_k = pltpu.make_async_copy(k_hbm, tr.at[0, 0], ld_sem.at[0])
    tr_v = pltpu.make_async_copy(v_hbm, tr.at[0, 1], ld_sem.at[1])
    q_lo = pltpu.make_async_copy(q_hbm.at[:, pl.ds(0, 512)], qv.at[0], ld_sem.at[2])
    q_hi = pltpu.make_async_copy(q_hbm.at[:, pl.ds(512, 512)], qv.at[1], ld_sem.at[3])

    @pl.when(driver)
    def _():
        own_k.start()
        own_v.start()

    @pl.when(foreign)
    def _():
        tr_k.start()
        tr_v.start()

    q_lo.start()
    q_hi.start()

    barrier = pltpu.get_barrier_semaphore()
    for dev in ((zu, t), (zd, t), (xr, t), (xl, t), (s, sib), (part, t), (part, sib)):
        pl.semaphore_signal(barrier, inc=1, device_id=dev, device_id_type=MESH)
    pl.semaphore_wait(barrier, 7)

    def remote(src, dst, send, recv, dev):
        return pltpu.make_async_remote_copy(
            src_ref=src, dst_ref=dst, send_sem=send, recv_sem=recv,
            device_id=dev, device_id_type=MESH)

    def blk(row, col):
        return kv.at[row, col]

    def zcopy(row, slot, dev):
        return remote(blk(row, x), blk(row, x), zs_sem.at[slot], kv_sem.at[row, x], (dev, t))

    def xcopy(n, j, row, col, dev):
        return remote(blk(row, col), blk(row, col), xs_sem.at[n, j], kv_sem.at[row, col], (dev, t))

    def dcopy(row, col):
        return remote(blk(row, col), blk(row, col), ds_sem.at[row, col], kv_sem.at[row, col], (s, sib))

    def arrived(row, col):
        pltpu.make_async_copy(blk(row, col), blk(row, col), kv_sem.at[row, col]).wait()

    def order(n):
        nu = rh + 2
        nd = 5 - rh
        m = jnp.minimum(nu, nd)
        k2 = (n + 1) // 2 - 1
        early = n <= 2 * m
        k = jnp.where(early, k2, n - 1 - m)
        from_u = jnp.where(early, lax.rem(n, 2), (nu > nd).astype(jnp.int32)) == 1
        row = jnp.where(from_u, rh + NZ - 1 - k, rh + 1 + k)
        row = jnp.where(n == 0, rh, lax.rem(row, NZ))
        return row, from_u

    xm1 = lax.rem(x + NX - 1, NX)
    xp1 = lax.rem(x + 1, NX)
    xp2 = lax.rem(x + 2, NX)

    def fwd_copies(n):
        row, from_u = order(n)
        even = lax.rem(row, 2) == 0
        return (even, xcopy(n, 2, row, xm1, xr), xcopy(n, 2, row, xp1, xl))

    def stage1(n, first):
        row, from_u = order(n)

        @pl.when(driver)
        def _():
            if first:
                @pl.when(pu < 5)
                def _():
                    zcopy(row, 0, zu).start()

                @pl.when(pd < 5)
                def _():
                    zcopy(row, 8, zd).start()
            else:
                arrived(row, x)

                @pl.when(jnp.logical_and(from_u, pu < 5))
                def _():
                    zcopy(row, n, zu).start()

                @pl.when(jnp.logical_and(jnp.logical_not(from_u), pd < 5))
                def _():
                    zcopy(row, n, zd).start()
            xcopy(n, 0, row, x, xr).start()
            xcopy(n, 1, row, x, xl).start()
            dcopy(row, x).start()

    def stage2(n):
        row, _ = order(n)

        @pl.when(driver)
        def _():
            even, right, left = fwd_copies(n)
            arrived(row, xm1)

            @pl.when(even)
            def _():
                right.start()
            dcopy(row, xm1).start()
            arrived(row, xp1)

            @pl.when(jnp.logical_not(even))
            def _():
                left.start()
            dcopy(row, xp1).start()

    def stage3(n):
        row, _ = order(n)

        @pl.when(driver)
        def _():
            arrived(row, xp2)
            dcopy(row, xp2).start()

        @pl.when(foreign)
        def _():
            for col in range(NX):
                arrived(row, col)

    own_down = remote(tr.at[0], kv.at[r, x], zs_sem.at[0], kv_sem.at[r, x], (zd, t))
    own_up = remote(tr.at[0], kv.at[r, x], zs_sem.at[0], kv_sem.at[r, x], (zu, t))
    hop_down = remote(tr.at[0], tr.at[1], zs_sem.at[0], tr_sem, (zd, t))
    hop_up = remote(tr.at[0], tr.at[1], zs_sem.at[0], tr_sem, (zu, t))
    fwd_down = remote(tr.at[1], kv.at[5, x], zs_sem.at[1], kv_sem.at[5, x], (zd, t))
    fwd_up = remote(tr.at[1], kv.at[6, x], zs_sem.at[1], kv_sem.at[6, x], (zu, t))

    q_sib = remote(qv.at[1], qin.at[0], qs_sem.at[0], q_sem.at[0], (s, sib))
    q_par = remote(qv.at[0], qin.at[1], qs_sem.at[0], q_sem.at[1], (part, t))
    q_pas = remote(qv.at[1], qin.at[1], qs_sem.at[1], q_sem.at[1], (part, sib))

    @pl.when(driver)
    def _():
        own_k.wait()
        own_v.wait()
        stage1(0, True)

    @pl.when(foreign)
    def _():
        tr_k.wait()
        tr_v.wait()
        for rr, cp in ((4, own_down), (5, hop_down), (6, hop_up), (7, own_up)):
            @pl.when(r == rr)
            def _():
                cp.start()

    q_lo.wait()
    q_hi.wait()

    @pl.when(driver)
    def _():
        q_sib.start()

    @pl.when(foreign)
    def _():
        q_par.start()
        q_pas.start()
        for rr, cp in ((4, fwd_down), (7, fwd_up)):
            @pl.when(r == rr)
            def _():
                pltpu.make_async_copy(tr.at[1], tr.at[1], tr_sem).wait()
                cp.start()

    acc[...] = jnp.zeros_like(acc)
    mrow[...] = jnp.full_like(mrow, NEG)

    def split(src, a):
        for h in range(4):
            f = src[:, h * HEAD:(h + 1) * HEAD].astype(jnp.float32) * LOG2_SCALE
            hi = f.astype(jnp.bfloat16)
            lo = (f - hi.astype(jnp.float32)).astype(jnp.bfloat16)
            qhl[a, h] = jnp.concatenate([hi, lo], axis=1)

    @pl.when(driver)
    def _():
        split(qv.at[0], 0)

    @pl.when(foreign)
    def _():
        pltpu.make_async_copy(qin.at[0], qin.at[0], q_sem.at[0]).wait()
        split(qin.at[0], 0)

    stage1(1, False)
    stage2(0)
    pltpu.make_async_copy(qin.at[1], qin.at[1], q_sem.at[1]).wait()
    split(qin.at[1], 1)

    def attend(a, row, pair, offset, masked):
        ks = kv[row, pl.ds(2 * pair, 2), 0].reshape(2 * ROWS, HEAD)
        vs = kv[row, pl.ds(2 * pair, 2), 1].reshape(2 * ROWS, HEAD)
        k2 = jnp.concatenate([ks, ks], axis=1)
        v1 = jnp.concatenate([vs, jnp.ones_like(vs)], axis=1)
        if masked:
            qpos = lax.broadcasted_iota(jnp.int32, (ROWS, 2 * ROWS), 0) + offset
            vis = qpos >= lax.broadcasted_iota(jnp.int32, (ROWS, 2 * ROWS), 1)
        qs = [qhl[a, h] for h in range(4)]
        ms = [mrow[a, h] for h in range(4)]

        def scores(h):
            sc = lax.dot_general(qs[h], k2, (((1,), (1,)), ((), ())),
                                 preferred_element_type=jnp.float32)
            return jnp.where(vis, sc, NEG) if masked else sc

        done = []
        cur = scores(0)
        for h in range(4):
            nxt = scores(h + 1) if h < 3 else None
            mn = jnp.maximum(ms[h], jnp.max(cur, axis=1, keepdims=True))
            al = jnp.exp2(ms[h] - mn)
            p = jnp.exp2(cur - jnp.concatenate([mn] * 4, axis=1)).astype(jnp.bfloat16)
            pv = jnp.dot(p, v1, preferred_element_type=jnp.float32)
            done.append((mn, al, pv))
            cur = nxt
        for h in range(4):
            mn, al, pv = done[h]
            mrow[a, h] = mn
            acc[a, h] = acc[a, h] * jnp.concatenate([al, al], axis=1) + pv

    def row_step(n, carry):
        @pl.when(n < NZ - 2)
        def _():
            stage1(n + 2, False)

        @pl.when(n < NZ - 1)
        def _():
            stage2(n + 1)

        stage3(n)
        row, _ = order(n)
        zr = row + ch * (NZ - 1 - 2 * row)

        def sub(i, carry2):
            a = i // 2
            pair = lax.rem(i, 2)
            bq = s + a * (part - s)
            pos = 2 * zr + pair

            @pl.when(pos < bq // 2)
            def _():
                attend(a, row, pair, 0, False)

            @pl.when(pos == bq // 2)
            def _():
                attend(a, row, pair, lax.rem(bq, 2) * ROWS, True)
            return carry2

        lax.fori_loop(0, 4, sub, 0)
        return carry

    lax.fori_loop(0, NZ, row_step, 0)

    for h in range(4):
        both = jnp.maximum(mrow[0, h], mrow[1, h])
        hm_ref[pl.ds(h, 1), :] = jnp.max(both, axis=0, keepdims=True) * math.log(2.0)
    hm_ref[pl.ds(4, 4), :] = jnp.zeros((4, 128), jnp.float32)

    for a in (1, 0):
        for h in range(4):
            res[a, :, pl.ds(h * HEAD, HEAD)] = (
                acc[a, h, :, :HEAD] / acc[a, h, :, HEAD:]).astype(jnp.bfloat16)

    lo_cols = o_hbm.at[:, pl.ds(0, 512)]
    hi_cols = o_hbm.at[:, pl.ds(512, 512)]
    back_d = remote(res.at[1], lo_cols, os_sem.at[1], o_sem.at[0], (part, t))
    back_s = remote(res.at[1], hi_cols, os_sem.at[1], o_sem.at[1], (part, sib))
    keep_d = pltpu.make_async_copy(res.at[0], lo_cols, os_sem.at[0])
    keep_s = remote(res.at[0], hi_cols, os_sem.at[0], o_sem.at[1], (s, sib))

    @pl.when(driver)
    def _():
        back_d.start()
        keep_d.start()

    @pl.when(foreign)
    def _():
        back_s.start()
        keep_s.start()

    @pl.when(driver)
    def _():
        @pl.when(pu < 5)
        def _():
            zcopy(r, 0, zu).wait_send()

        @pl.when(pd < 5)
        def _():
            zcopy(r, 8, zd).wait_send()

        def drain(n, carry):
            row, from_u = order(n)

            @pl.when(jnp.logical_and(n > 0, jnp.logical_and(from_u, pu < 5)))
            def _():
                zcopy(row, n, zu).wait_send()

            @pl.when(jnp.logical_and(n > 0, jnp.logical_and(jnp.logical_not(from_u), pd < 5)))
            def _():
                zcopy(row, n, zd).wait_send()
            xcopy(n, 0, row, x, xr).wait_send()
            xcopy(n, 1, row, x, xl).wait_send()
            xcopy(n, 2, row, xm1, xr).wait_send()
            for col in range(NX):
                dcopy(row, col).wait_send()
            return carry

        lax.fori_loop(0, NZ, drain, 0)
        q_sib.wait_send()
        back_d.wait_send()
        keep_d.wait()
        keep_s.wait_recv()

    @pl.when(foreign)
    def _():
        own_down.wait_send()

        @pl.when(jnp.logical_or(r == 4, r == 7))
        def _():
            fwd_down.wait_send()
        q_par.wait_send()
        q_pas.wait_send()
        back_s.wait_send()
        keep_s.wait_send()
        back_d.wait_recv()
        back_s.wait_recv()


def attend_all(q, k, v):
    bf = jnp.bfloat16
    return pl.pallas_call(
        attention_kernel,
        out_shape=(jax.ShapeDtypeStruct((ROWS, 1024), bf),
                   jax.ShapeDtypeStruct((8, 128), jnp.float32)),
        in_specs=[pl.BlockSpec(memory_space=pl.ANY)] * 3,
        out_specs=(pl.BlockSpec(memory_space=pl.ANY),
                   pl.BlockSpec(memory_space=pltpu.VMEM)),
        scratch_shapes=[
            pltpu.VMEM((2, ROWS, 512), bf),
            pltpu.VMEM((NZ, NX, 2, ROWS, HEAD), bf),
            pltpu.VMEM((2, 2, ROWS, HEAD), bf),
            pltpu.VMEM((2, ROWS, 512), bf),
            pltpu.VMEM((2, 4, ROWS, 256), bf),
            pltpu.VMEM((2, 4, ROWS, 256), jnp.float32),
            pltpu.VMEM((2, 4, ROWS, 128), jnp.float32),
            pltpu.VMEM((2, ROWS, 512), bf),
            pltpu.SemaphoreType.DMA((4,)),
            pltpu.SemaphoreType.DMA((NZ, NX)),
            pltpu.SemaphoreType.DMA,
            pltpu.SemaphoreType.DMA((2,)),
            pltpu.SemaphoreType.DMA((2,)),
            pltpu.SemaphoreType.DMA((9,)),
            pltpu.SemaphoreType.DMA((NZ, 3)),
            pltpu.SemaphoreType.DMA((NZ, NX)),
            pltpu.SemaphoreType.DMA((2,)),
            pltpu.SemaphoreType.DMA((2,)),
        ],
        compiler_params=pltpu.CompilerParams(
            collective_id=0, has_side_effects=True, vmem_limit_bytes=48 * 2**20),
        name="attend",
    )(q, k, v)


def shards(q, k, v, w, kw):
    heads, groups, per = 64, 8, 8
    s = lax.axis_index("seq")
    t = lax.axis_index("tp")
    out, hm = attend_all(q, k, v)
    ch = s // 16
    c = t % 2
    base = (t - c + ch) * per + 4 * (c != ch).astype(jnp.int32)
    vec = lax.dynamic_update_slice(jnp.full((heads,), -3e38, jnp.float32), hm[:4, 0], (base,))
    head_max = lax.pmax(vec, ("seq", "tp"))
    clip = TAU / jnp.maximum(head_max.reshape(groups, per).max(1), TAU)
    own_max = lax.dynamic_slice(head_max, (t * per,), (per,))
    own_clip = lax.dynamic_slice(clip, (t,), (1,))
    factor = (TAU / jnp.maximum(own_max, TAU)) / jnp.sqrt(own_clip)
    w_out = (w.astype(jnp.float32) * jnp.repeat(factor, HEAD)[None, :]).astype(jnp.bfloat16)
    k_out = (kw.astype(jnp.float32) * jnp.repeat(jnp.sqrt(clip), HEAD)[None, :]).astype(jnp.bfloat16)
    return out, own_max, w_out, k_out


def solution(mesh):
    in_specs = (P("seq", "tp"), P("seq", "tp"), P("seq", "tp"), P("seq", "tp"), P("seq", None))
    out_specs = (P("seq", "tp"), P("tp"), P("seq", "tp"), P("seq", None))
    return jax.shard_map(shards, mesh=mesh, in_specs=in_specs, out_specs=out_specs, check_vma=False)
```

time: 209 us -> 160 us (0.77)
  waiting for transfers between devices: 96.5 us -> 0 us
  blocking collectives: 0 us -> 87.7 us
  Pallas kernels: 0 us -> 60.5 us
  starting transfers between devices: 54.8 us -> 0 us
  between operations: 14.9 us -> 1.38 us
  other arithmetic: 13.9 us -> 2.98 us
  local copies, waits for them, and re-layouts: 12.7 us -> 4.65 us
  matrix products: 7.96 us -> 0 us
  loops' own time: 5.66 us -> 0 us
    pmax x0 -> x1, blocking collectives: none -> 87.7 us  [shards(): head_max = lax.pmax(vec, ('seq', 'tp'))]
    all_gather x1 -> x0, waiting for transfers between devices: 84.7 us -> none  [in_one_piece(): lax.all_gather(both, axis, axis=dim, tiled=True)]
    pallas_call x0 -> x1, Pallas kernels: none -> 60.5 us  [attend_all(): pl.pallas_call(attention_kernel, out_shape=(jax.ShapeDtypeStruct((ROWS, 1...]
    all_to_all x2 -> x0, starting transfers between devices: 54.8 us -> none  [sent_to_all(): lax.all_to_all(jnp.broadcast_to(value[None], (count, *value.shape)), axis...]
    all_to_all x2 -> x0, waiting for transfers between devices: 11.7 us -> none  [sent_to_all(): lax.all_to_all(jnp.broadcast_to(value[None], (count, *value.shape)), axis...]
    dot_general x4 -> x0, matrix products: 7.96 us -> none  [the longest x2 5.25 us: attend_block(): jnp.einsum('rkgn,nkd->rkgd', expo.astype(jnp.bfloat16), value_heads_view,...]
    reduce_max x4 -> x1, other arithmetic: 7.58 us -> 0.12 us  [shards(): clip = TAU / jnp.maximum(head_max.reshape(groups, per).max(1), TAU)]
    another operation x9 -> x0, loops' own time: 5.66 us -> none  [the longest x1 5.43 us: shards(): lax.fori_loop(0, piece_rows // block_rows, one_block, (fresh_state(), fre...]
  transfers between devices with their start and end apart: 3 -> 0, of which waited for: 3 -> 0; matrix products, arithmetic and copies ran while one was open for 2% -> 0% of each run, Pallas kernels for 0% -> 0%
where the time goes in v1:
time: 160 us; the launch traced here: 157 us
  blocking collectives  87.7 us (55%)
  Pallas kernels  60.5 us (38%)
  local copies, waits for them, and re-layouts  4.65 us (3%)
  other arithmetic  2.98 us (2%)
    pmax x1, blocking collectives, shards(): head_max = lax.pmax(vec, ('seq', 'tp'))  87.7 us
    pallas_call x1, Pallas kernels, attend_all(): pl.pallas_call(attention_kernel, out_shape=(jax.ShapeDtypeStruct((ROWS, 1...  60.5 us
    unnamed x9, local copies, waits for them, and re-layouts  3.48 us

profile of v1, /device:TPU:32, one launch (start us, length us, event | category | flops | bytes accessed | tf_op | source)
XLA Modules:
  0.0 157.2 jit_solution(12453247401576297266)
XLA Ops:
  0.6 0.0 copy-start.1
  0.7 0.8 copy-done.1
  1.5 0.0 copy-start
  1.5 1.0 copy-done
  2.5 0.0 copy-start.2
  2.5 0.8 copy-done.2
  3.4 0.0 copy-start.3
  3.4 60.5 %attend.1 = (bf16[256,1024]{1,0:T(8,128)(2,1)S(1)}, f32[8,128]{1,0:T(8,128)S(1)}) custom-call(bf16[256,1024]{1,0:T(8,128)(2,1)S(1)} %copy-done, bf16[256,128]{1,0:T(8,128)(2,1)S(1)} %copy-done.1, bf16[256,128]{1,0:T(8,128)(2,1)S(1)} %copy-done.2), custom_call_target="tpu_custom_call" | custom-call | tf_op jit(solution)/shard_map/attend/pallas_call | solution.py:377
  63.9 0.1 slice_reduce_fusion
  64.0 0.2 dynamic_update_slice.3
  64.3 87.7 %pmax.7 = f32[64]{0:T(128)S(1)} all-reduce(f32[64]{0:T(128)S(1)} %dynamic_update_slice.3), channel_id=1, replica_groups=mesh['seq'=32,'tp'=8] {'seq','tp'}, use_global_device_ids=true, to_apply=%region_0.1 | all-reduce | flops 64 | bytes 512 | tf_op jit(solution)/shard_map/pmax | solution.py:419
  152.0 0.1 reshape.13
  152.0 0.1 reduce_max.9
  152.2 0.6 dynamic_slice.7
  153.5 0.6 multiply_divide_fusion
  154.1 0.1 broadcast_bitcast_fusion.1
  154.1 0.1 broadcast_bitcast_fusion
  154.2 0.0 copy-done.3
  154.2 2.3 %multiply_convert_fusion = (bf16[256,1024]{1,0:T(8,128)(2,1)}, bf16[256,1024]{1,0:T(8,128)(2,1)}) fusion(bf16[256,1024]{1,0:T(8,128)(2,1)S(1)} %copy-done.3, f32[1024]{0:T(1024)S(1)} %broadcast_bitcast_fusion, f32[1024]{0:T(1024)S(1)} %broadcast_bitcast_fusion.1, bf16[256,1024]{1,0:T(8,128)(2,1)} %param.8), kind=kLoop, calls=%fused_computation | loop fusion | flops 1572864 | bytes 2105344 | tf_op jit(solution)/shard_map/convert_element_type | solution.py:425
  156.5 0.8 copy.11
  (2 shorter events, 0.0 us)
Async XLA Ops:
  0.6 0.8 copy-start.1
  1.5 1.0 copy-start
  2.5 0.8 copy-start.2
  3.4 150.8 %copy-start.3 = (bf16[256,1024]{1,0:T(8,128)(2,1)S(1)}, bf16[256,1024]{1,0:T(8,128)(2,1)}, u32[]{:S(2)}) copy-start(bf16[256,1024]{1,0:T(8,128)(2,1)} %param.9) | copy-start | bytes 1572868

commit v2 on v1

--- a/solution.py
+++ b/solution.py
@@ -19,7 +19,8 @@
 def attention_kernel(q_hbm, k_hbm, v_hbm, o_hbm, hm_ref,
                      qv, kv, tr, qin, qhl, acc, mrow, res,
                      ld_sem, kv_sem, tr_sem, q_sem, o_sem,
-                     zs_sem, xs_sem, ds_sem, qs_sem, os_sem):
+                     zs_sem, xs_sem, ds_sem, qs_sem, os_sem,
+                     mx_out, mx_in, ms_sem, mr_sem):
     s = lax.axis_index("seq")
     t = lax.axis_index("tp")
     z = s // NX
@@ -62,9 +63,18 @@
     q_hi.start()
 
     barrier = pltpu.get_barrier_semaphore()
-    for dev in ((zu, t), (zd, t), (xr, t), (xl, t), (s, sib), (part, t), (part, sib)):
+    row_peers, ring_peers, y_peers = [(s, sib)], [], []
+    for d in range(1, NX):
+        at = z * NX + lax.rem(x + d, NX)
+        row_peers += [(at, t), (at, sib)]
+    for d in range(1, NZ):
+        ring_peers.append((lax.rem(z + d, NZ) * NX + x, t))
+    for d in range(1, 4):
+        y_peers.append((s, lax.rem(t + 2 * d, 8)))
+    everyone = row_peers + ring_peers + y_peers + [(part, t), (part, sib)]
+    for dev in everyone:
         pl.semaphore_signal(barrier, inc=1, device_id=dev, device_id_type=MESH)
-    pl.semaphore_wait(barrier, 7)
+    pl.semaphore_wait(barrier, len(everyone))
 
     def remote(src, dst, send, recv, dev):
         return pltpu.make_async_remote_copy(
@@ -297,10 +307,14 @@
 
     lax.fori_loop(0, NZ, row_step, 0)
 
+    lane = lax.broadcasted_iota(jnp.int32, (8, 128), 1)
+    base = (t - c + ch) * 8 + 4 * (1 - (c == ch).astype(jnp.int32))
+    best = jnp.full((8, 128), -3e38, jnp.float32)
     for h in range(4):
         both = jnp.maximum(mrow[0, h], mrow[1, h])
-        hm_ref[pl.ds(h, 1), :] = jnp.max(both, axis=0, keepdims=True) * math.log(2.0)
-    hm_ref[pl.ds(4, 4), :] = jnp.zeros((4, 128), jnp.float32)
+        top = jnp.max(both, axis=0, keepdims=True) * math.log(2.0)
+        best = jnp.where(lane == base + h, jnp.broadcast_to(top, (8, 128)), best)
+    mx_out[0] = best
 
     for a in (1, 0):
         for h in range(4):
@@ -323,6 +337,23 @@
     def _():
         back_s.start()
         keep_s.start()
+
+    at = 0
+    for rnd, peers in enumerate((row_peers, ring_peers, y_peers)):
+        sends = [remote(mx_out.at[rnd], mx_in.at[at + i], ms_sem.at[at + i], mr_sem.at[at + i], dev)
+                 for i, dev in enumerate(peers)]
+        for cp in sends:
+            cp.start()
+        best = mx_out[rnd]
+        for i, cp in enumerate(sends):
+            cp.wait_recv()
+            best = jnp.maximum(best, mx_in[at + i])
+        if rnd < 2:
+            mx_out[rnd + 1] = best
+        at += len(peers)
+    for i in range(at):
+        remote(mx_out.at[0], mx_in.at[i], ms_sem.at[i], mr_sem.at[i], (s, sib)).wait_send()
+    hm_ref[...] = jnp.broadcast_to(best[0:1], (128, 128)).T
 
     @pl.when(driver)
     def _():
@@ -377,7 +408,7 @@
     return pl.pallas_call(
         attention_kernel,
         out_shape=(jax.ShapeDtypeStruct((ROWS, 1024), bf),
-                   jax.ShapeDtypeStruct((8, 128), jnp.float32)),
+                   jax.ShapeDtypeStruct((128, 128), jnp.float32)),
         in_specs=[pl.BlockSpec(memory_space=pl.ANY)] * 3,
         out_specs=(pl.BlockSpec(memory_space=pl.ANY),
                    pl.BlockSpec(memory_space=pltpu.VMEM)),
@@ -400,30 +431,48 @@
             pltpu.SemaphoreType.DMA((NZ, NX)),
             pltpu.SemaphoreType.DMA((2,)),
             pltpu.SemaphoreType.DMA((2,)),
+            pltpu.VMEM((3, 8, 128), jnp.float32),
+            pltpu.VMEM((17, 8, 128), jnp.float32),
+            pltpu.SemaphoreType.DMA((17,)),
+            pltpu.SemaphoreType.DMA((17,)),
         ],
         compiler_params=pltpu.CompilerParams(
-            collective_id=0, has_side_effects=True, vmem_limit_bytes=48 * 2**20),
+            collective_id=0, has_side_effects=True, vmem_limit_bytes=67043328),
         name="attend",
     )(q, k, v)
 
 
+def scale_kernel(hm_ref, w_ref, kw_ref, wo_ref, ko_ref, top_ref):
+    t = lax.axis_index("tp")
+    for g in range(8):
+        most = jnp.max(hm_ref[pl.ds(8 * g, 8), :], axis=0, keepdims=True)
+        f = jnp.sqrt(TAU / jnp.maximum(most, TAU))
+        cols = slice(g * HEAD, (g + 1) * HEAD)
+        ko_ref[:, cols] = (kw_ref[:, cols].astype(jnp.float32) * f).astype(jnp.bfloat16)
+    mine = hm_ref[pl.ds(pl.multiple_of(8 * t, 8), 8), :]
+    top_ref[...] = mine
+    root = jnp.sqrt(TAU / jnp.maximum(jnp.max(mine, axis=0, keepdims=True), TAU))
+    gamma = (TAU / jnp.maximum(mine, TAU)) / root
+    for h in range(8):
+        cols = slice(h * HEAD, (h + 1) * HEAD)
+        wo_ref[:, cols] = (w_ref[:, cols].astype(jnp.float32) * gamma[h:h + 1]).astype(jnp.bfloat16)
+
+
+def scale(hm, w, kw):
+    vm = pl.BlockSpec(memory_space=pltpu.VMEM)
+    return pl.pallas_call(
+        scale_kernel,
+        out_shape=(jax.ShapeDtypeStruct(w.shape, w.dtype),
+                   jax.ShapeDtypeStruct(kw.shape, kw.dtype),
+                   jax.ShapeDtypeStruct((8, 128), jnp.float32)),
+        in_specs=[vm] * 3, out_specs=(vm,) * 3, name="scale",
+    )(hm, w, kw)
+
+
 def shards(q, k, v, w, kw):
-    heads, groups, per = 64, 8, 8
-    s = lax.axis_index("seq")
-    t = lax.axis_index("tp")
     out, hm = attend_all(q, k, v)
-    ch = s // 16
-    c = t % 2
-    base = (t - c + ch) * per + 4 * (c != ch).astype(jnp.int32)
-    vec = lax.dynamic_update_slice(jnp.full((heads,), -3e38, jnp.float32), hm[:4, 0], (base,))
-    head_max = lax.pmax(vec, ("seq", "tp"))
-    clip = TAU / jnp.maximum(head_max.reshape(groups, per).max(1), TAU)
-    own_max = lax.dynamic_slice(head_max, (t * per,), (per,))
-    own_clip = lax.dynamic_slice(clip, (t,), (1,))
-    factor = (TAU / jnp.maximum(own_max, TAU)) / jnp.sqrt(own_clip)
-    w_out = (w.astype(jnp.float32) * jnp.repeat(factor, HEAD)[None, :]).astype(jnp.bfloat16)
-    k_out = (kw.astype(jnp.float32) * jnp.repeat(jnp.sqrt(clip), HEAD)[None, :]).astype(jnp.bfloat16)
-    return out, own_max, w_out, k_out
+    w_out, k_out, top = scale(hm, w, kw)
+    return out, top[:, 0], w_out, k_out
 
 
 def solution(mesh):

time: 160 us -> 82.7 us (0.52)
  blocking collectives: 87.7 us -> 0 us
  Pallas kernels: 60.5 us -> 78.6 us
  other arithmetic: 2.98 us -> 0 us
  local copies, waits for them, and re-layouts: 4.65 us -> 2.11 us
    pmax x1 -> x0, blocking collectives: 87.7 us -> none  [shards(): head_max = lax.pmax(vec, ('seq', 'tp'))]
    pallas_call x1, Pallas kernels: 60.5 us -> 76.1 us  [attend_all(): pl.pallas_call(attention_kernel, out_shape=(jax.ShapeDtypeStruct((ROWS, 1...]
    pallas_call x0 -> x1, Pallas kernels: none -> 2.46 us  [scale(): pl.pallas_call(scale_kernel, out_shape=(jax.ShapeDtypeStruct(w.shape, w.d...]
    convert_element_type x1 -> x0, other arithmetic: 2.26 us -> none  [shards(): (kw.astype(jnp.float32) * jnp.repeat(jnp.sqrt(clip), HEAD)[None, :]).asty...]
    unnamed x9 -> x5, local copies, waits for them, and re-layouts: 3.48 us -> 1.48 us
where the time goes in v2:
time: 82.7 us; the launch traced here: 81.3 us
  Pallas kernels  78.6 us (95%)
  local copies, waits for them, and re-layouts  2.11 us (3%)
    pallas_call x1, Pallas kernels, attend_all(): pl.pallas_call(attention_kernel, out_shape=(jax.ShapeDtypeStruct((ROWS, 1...  76.1 us
    pallas_call x1, Pallas kernels, scale(): pl.pallas_call(scale_kernel, out_shape=(jax.ShapeDtypeStruct(w.shape, w.d...  2.46 us

profile of v2, /device:TPU:32, one launch (start us, length us, event | category | flops | bytes accessed | tf_op | source)
XLA Modules:
  0.0 81.3 jit_solution(15859660763393297887)
XLA Ops:
  0.6 76.1 %attend.1 = (bf16[256,1024]{1,0:T(8,128)(2,1)}, f32[128,128]{1,0:T(8,128)}) custom-call(bf16[256,1024]{1,0:T(8,128)(2,1)} %q_hbm.1, bf16[256,128]{1,0:T(8,128)(2,1)} %k_hbm.1, bf16[256,128]{1,0:T(8,128)(2,1)} %v_hbm.1), custom_call_target="tpu_custom_call" | custom-call | tf_op jit(solution)/shard_map/attend/pallas_call | solution.py:408
  76.8 0.0 copy-start
  76.8 2.5 %scale.1 = (bf16[256,1024]{1,0:T(8,128)(2,1)}, bf16[256,1024]{1,0:T(8,128)(2,1)}, f32[8,128]{1,0:T(8,128)}) custom-call(f32[128,128]{1,0:T(8,128)} %get-tuple-element.10.hm_ref, bf16[256,1024]{1,0:T(8,128)(2,1)} %w_ref.1, bf16[256,1024]{1,0:T(8,128)(2,1)} %kw_ref.1), custom_call_target="tpu_custom_call" | custom-call | tf_op jit(solution)/shard_map/scale/pallas_call | solution.py:463
  79.2 0.0 copy-start.1
  79.2 0.7 copy-done.1
  79.9 0.6 slice_reduce_fusion
  80.5 0.0 copy-done
  80.5 0.8 copy.10
Async XLA Ops:
  76.8 3.8 %copy-start = (bf16[256,1024]{1,0:T(8,128)(2,1)S(1)}, bf16[256,1024]{1,0:T(8,128)(2,1)}, u32[]{:S(2)}) copy-start(bf16[256,1024]{1,0:T(8,128)(2,1)} %get-tuple-element.18) | copy-start | bytes 1572868
  79.2 0.7 copy-start.1

commit v3 on v2

--- a/solution.py
+++ b/solution.py
@@ -12,6 +12,8 @@
 NZ, NX = 8, 4
 TAU = 10.0
 NEG = -1e30
+LAG = 3
+LEAD1, LEAD2 = 6, 3
 LOG2_SCALE = math.log2(math.e) / math.sqrt(128.0)
 MESH = pl.DeviceIdType.MESH
 
@@ -32,7 +34,7 @@
     r = z + c * (NZ - 1 - 2 * z)
     rh = z + ch * (NZ - 1 - 2 * z)
     sib = t + 1 - 2 * c
-    part = (NZ - 1 - z) * NX + (NX - 1 - x)
+    part = (NZ - 1 - z) * NX + x
     xr = z * NX + lax.rem(x + 1, NX)
     xl = z * NX + lax.rem(x + NX - 1, NX)
     zu_z = lax.rem(z + NZ + 1 - 2 * c, NZ)
@@ -211,13 +213,13 @@
 
     @pl.when(foreign)
     def _():
+        for rr, cp in ((4, fwd_down), (7, fwd_up)):
+            @pl.when(r == rr)
+            def _():
+                pltpu.make_async_copy(tr.at[1], tr.at[1], tr_sem).wait()
+                cp.start()
         q_par.start()
         q_pas.start()
-        for rr, cp in ((4, fwd_down), (7, fwd_up)):
-            @pl.when(r == rr)
-            def _():
-                pltpu.make_async_copy(tr.at[1], tr.at[1], tr_sem).wait()
-                cp.start()
 
     acc[...] = jnp.zeros_like(acc)
     mrow[...] = jnp.full_like(mrow, NEG)
@@ -238,10 +240,15 @@
         pltpu.make_async_copy(qin.at[0], qin.at[0], q_sem.at[0]).wait()
         split(qin.at[0], 0)
 
-    stage1(1, False)
-    stage2(0)
-    pltpu.make_async_copy(qin.at[1], qin.at[1], q_sem.at[1]).wait()
-    split(qin.at[1], 1)
+    def early(n, carry):
+        stage1(n, False)
+
+        @pl.when(n >= LEAD1 - LEAD2)
+        def _():
+            stage2(n - (LEAD1 - LEAD2))
+        return carry
+
+    lax.fori_loop(1, LEAD1, early, 0)
 
     def attend(a, row, pair, offset, masked):
         ks = kv[row, pl.ds(2 * pair, 2), 0].reshape(2 * ROWS, HEAD)
@@ -249,10 +256,11 @@
         k2 = jnp.concatenate([ks, ks], axis=1)
         v1 = jnp.concatenate([vs, jnp.ones_like(vs)], axis=1)
         if masked:
-            qpos = lax.broadcasted_iota(jnp.int32, (ROWS, 2 * ROWS), 0) + offset
-            vis = qpos >= lax.broadcasted_iota(jnp.int32, (ROWS, 2 * ROWS), 1)
-        qs = [qhl[a, h] for h in range(4)]
-        ms = [mrow[a, h] for h in range(4)]
+            qpos = lax.broadcasted_iota(jnp.int32, (2 * ROWS, 2 * ROWS), 0)
+            qpos = (qpos & (ROWS - 1)) + offset
+            vis = qpos >= lax.broadcasted_iota(jnp.int32, (2 * ROWS, 2 * ROWS), 1)
+        qs = [qhl[a, pl.ds(2 * h, 2)].reshape(2 * ROWS, 256) for h in range(2)]
+        ms = [mrow[a, pl.ds(2 * h, 2)].reshape(2 * ROWS, 128) for h in range(2)]
 
         def scores(h):
             sc = lax.dot_general(qs[h], k2, (((1,), (1,)), ((), ())),
@@ -261,43 +269,54 @@
 
         done = []
         cur = scores(0)
-        for h in range(4):
-            nxt = scores(h + 1) if h < 3 else None
+        for h in range(2):
+            nxt = scores(h + 1) if h < 1 else None
             mn = jnp.maximum(ms[h], jnp.max(cur, axis=1, keepdims=True))
             al = jnp.exp2(ms[h] - mn)
             p = jnp.exp2(cur - jnp.concatenate([mn] * 4, axis=1)).astype(jnp.bfloat16)
             pv = jnp.dot(p, v1, preferred_element_type=jnp.float32)
             done.append((mn, al, pv))
             cur = nxt
-        for h in range(4):
+        for h in range(2):
             mn, al, pv = done[h]
-            mrow[a, h] = mn
-            acc[a, h] = acc[a, h] * jnp.concatenate([al, al], axis=1) + pv
+            two = pl.ds(2 * h, 2)
+            mrow[a, two] = mn.reshape(2, ROWS, 128)
+            old = acc[a, two].reshape(2 * ROWS, 256)
+            acc[a, two] = (old * jnp.concatenate([al, al], axis=1) + pv).reshape(2, ROWS, 256)
 
     def row_step(n, carry):
-        @pl.when(n < NZ - 2)
-        def _():
-            stage1(n + 2, False)
-
-        @pl.when(n < NZ - 1)
-        def _():
-            stage2(n + 1)
-
-        stage3(n)
-        row, _ = order(n)
-        zr = row + ch * (NZ - 1 - 2 * row)
+        @pl.when(n < NZ - LEAD1)
+        def _():
+            stage1(n + LEAD1, False)
+
+        @pl.when(n < NZ - LEAD2)
+        def _():
+            stage2(n + LEAD2)
+
+        @pl.when(n < NZ)
+        def _():
+            stage3(n)
+
+        @pl.when(n == LAG)
+        def _():
+            pltpu.make_async_copy(qin.at[1], qin.at[1], q_sem.at[1]).wait()
+            split(qin.at[1], 1)
 
         def sub(i, carry2):
             a = i // 2
             pair = lax.rem(i, 2)
+            m = n - LAG * a
+            live = jnp.logical_and(m >= 0, m < NZ)
+            row, _ = order(jnp.clip(m, 0, NZ - 1))
+            zr = row + ch * (NZ - 1 - 2 * row)
             bq = s + a * (part - s)
             pos = 2 * zr + pair
 
-            @pl.when(pos < bq // 2)
+            @pl.when(jnp.logical_and(live, pos < bq // 2))
             def _():
                 attend(a, row, pair, 0, False)
 
-            @pl.when(pos == bq // 2)
+            @pl.when(jnp.logical_and(live, pos == bq // 2))
             def _():
                 attend(a, row, pair, lax.rem(bq, 2) * ROWS, True)
             return carry2
@@ -305,7 +324,7 @@
         lax.fori_loop(0, 4, sub, 0)
         return carry
 
-    lax.fori_loop(0, NZ, row_step, 0)
+    lax.fori_loop(0, NZ + LAG, row_step, 0)
 
     lane = lax.broadcasted_iota(jnp.int32, (8, 128), 1)
     base = (t - c + ch) * 8 + 4 * (1 - (c == ch).astype(jnp.int32))

time: 82.7 us -> 72 us (0.87); the launches traced: 81.3 us -> 71.9 us
  Pallas kernels: 78.6 us -> 69.2 us
    pallas_call x1, Pallas kernels: 76.1 us -> 66.7 us  [attend_all(): pl.pallas_call(attention_kernel, out_shape=(jax.ShapeDtypeStruct((ROWS, 1...]
where the time goes in v3:
time: 72 us; the launch traced here: 71.9 us
  Pallas kernels  69.2 us (96%)
  local copies, waits for them, and re-layouts  2.11 us (3%)
    pallas_call x1, Pallas kernels, attend_all(): pl.pallas_call(attention_kernel, out_shape=(jax.ShapeDtypeStruct((ROWS, 1...  66.7 us
    pallas_call x1, Pallas kernels, scale(): pl.pallas_call(scale_kernel, out_shape=(jax.ShapeDtypeStruct(w.shape, w.d...  2.46 us
    unnamed x5, local copies, waits for them, and re-layouts  1.48 us

profile of v3, /device:TPU:32, one launch (start us, length us, event | category | flops | bytes accessed | tf_op | source)
XLA Modules:
  0.0 71.9 jit_solution(8961664197783138194)
XLA Ops:
  0.6 66.7 %attend.1 = (bf16[256,1024]{1,0:T(8,128)(2,1)}, f32[128,128]{1,0:T(8,128)}) custom-call(bf16[256,1024]{1,0:T(8,128)(2,1)} %q_hbm.1, bf16[256,128]{1,0:T(8,128)(2,1)} %k_hbm.1, bf16[256,128]{1,0:T(8,128)(2,1)} %v_hbm.1), custom_call_target="tpu_custom_call" | custom-call | tf_op jit(solution)/shard_map/attend/pallas_call | solution.py:427
  67.3 0.0 copy-start
  67.3 2.5 %scale.1 = (bf16[256,1024]{1,0:T(8,128)(2,1)}, bf16[256,1024]{1,0:T(8,128)(2,1)}, f32[8,128]{1,0:T(8,128)}) custom-call(f32[128,128]{1,0:T(8,128)} %get-tuple-element.10.hm_ref, bf16[256,1024]{1,0:T(8,128)(2,1)} %w_ref.1, bf16[256,1024]{1,0:T(8,128)(2,1)} %kw_ref.1), custom_call_target="tpu_custom_call" | custom-call | tf_op jit(solution)/shard_map/scale/pallas_call | solution.py:482
  69.8 0.0 copy-start.1
  69.8 0.7 copy-done.1
  70.5 0.6 slice_reduce_fusion
  71.1 0.0 copy-done
  71.1 0.8 %copy.10 = bf16[256,1024]{1,0:T(8,128)(2,1)} copy(bf16[256,1024]{1,0:T(8,128)(2,1)S(1)} %copy-done) | data formatting | bytes 1048576
Async XLA Ops:
  67.3 3.8 %copy-start = (bf16[256,1024]{1,0:T(8,128)(2,1)S(1)}, bf16[256,1024]{1,0:T(8,128)(2,1)}, u32[]{:S(2)}) copy-start(bf16[256,1024]{1,0:T(8,128)(2,1)} %get-tuple-element.18) | copy-start | bytes 1572868
  69.8 0.7 copy-start.1

commit v4 on v3

--- a/solution.py
+++ b/solution.py
@@ -12,8 +12,8 @@
 NZ, NX = 8, 4
 TAU = 10.0
 NEG = -1e30
-LAG = 3
-LEAD1, LEAD2 = 6, 3
+LATE = 3
+LEAD1, LEAD2 = 4, 2
 LOG2_SCALE = math.log2(math.e) / math.sqrt(128.0)
 MESH = pl.DeviceIdType.MESH
 
@@ -297,16 +297,18 @@
         def _():
             stage3(n)
 
-        @pl.when(n == LAG)
+        @pl.when(n == LATE)
         def _():
             pltpu.make_async_copy(qin.at[1], qin.at[1], q_sem.at[1]).wait()
             split(qin.at[1], 1)
 
         def sub(i, carry2):
-            a = i // 2
+            a = (i >= 2).astype(jnp.int32)
             pair = lax.rem(i, 2)
-            m = n - LAG * a
-            live = jnp.logical_and(m >= 0, m < NZ)
+            last = jnp.minimum(n, 2 * (n - LATE) + 1)
+            from_row = jnp.maximum(jnp.minimum(n - 1, 2 * (n - LATE) - 1) + 1, 0)
+            m = jnp.where(i < 2, n, from_row + i // 2 - 1)
+            live = m <= jnp.where(i < 2, n, last)
             row, _ = order(jnp.clip(m, 0, NZ - 1))
             zr = row + ch * (NZ - 1 - 2 * row)
             bq = s + a * (part - s)
@@ -321,10 +323,10 @@
                 attend(a, row, pair, lax.rem(bq, 2) * ROWS, True)
             return carry2
 
-        lax.fori_loop(0, 4, sub, 0)
+        lax.fori_loop(0, 6, sub, 0)
         return carry
 
-    lax.fori_loop(0, NZ + LAG, row_step, 0)
+    lax.fori_loop(0, NZ, row_step, 0)
 
     lane = lax.broadcasted_iota(jnp.int32, (8, 128), 1)
     base = (t - c + ch) * 8 + 4 * (1 - (c == ch).astype(jnp.int32))
@@ -461,37 +463,61 @@
     )(q, k, v)
 
 
-def scale_kernel(hm_ref, w_ref, kw_ref, wo_ref, ko_ref, top_ref):
+def scale_kernel(hm_ref, w_hbm, kw_hbm, att_hbm, wo_hbm, ko_hbm, ao_hbm, top_ref,
+                 w_v, kw_v, att_v, in_sem, out_sem):
     t = lax.axis_index("tp")
+    loads = [pltpu.make_async_copy(src, dst, in_sem.at[i]) for i, (src, dst) in enumerate(
+        ((kw_hbm, kw_v), (w_hbm, w_v), (att_hbm, att_v)))]
+    stores = [pltpu.make_async_copy(src, dst, out_sem.at[i]) for i, (src, dst) in enumerate(
+        ((kw_v, ko_hbm), (w_v, wo_hbm), (att_v, ao_hbm)))]
+    for cp in loads:
+        cp.start()
+    mine = hm_ref[pl.ds(pl.multiple_of(8 * t, 8), 8), :]
+    root = jnp.sqrt(TAU / jnp.maximum(jnp.max(mine, axis=0, keepdims=True), TAU))
+    gamma = (TAU / jnp.maximum(mine, TAU)) / root
+    clips = []
     for g in range(8):
         most = jnp.max(hm_ref[pl.ds(8 * g, 8), :], axis=0, keepdims=True)
-        f = jnp.sqrt(TAU / jnp.maximum(most, TAU))
+        clips.append(jnp.sqrt(TAU / jnp.maximum(most, TAU)))
+    loads[0].wait()
+    for g in range(8):
         cols = slice(g * HEAD, (g + 1) * HEAD)
-        ko_ref[:, cols] = (kw_ref[:, cols].astype(jnp.float32) * f).astype(jnp.bfloat16)
-    mine = hm_ref[pl.ds(pl.multiple_of(8 * t, 8), 8), :]
-    top_ref[...] = mine
-    root = jnp.sqrt(TAU / jnp.maximum(jnp.max(mine, axis=0, keepdims=True), TAU))
-    gamma = (TAU / jnp.maximum(mine, TAU)) / root
+        kw_v[:, cols] = (kw_v[:, cols].astype(jnp.float32) * clips[g]).astype(jnp.bfloat16)
+    stores[0].start()
+    loads[1].wait()
     for h in range(8):
         cols = slice(h * HEAD, (h + 1) * HEAD)
-        wo_ref[:, cols] = (w_ref[:, cols].astype(jnp.float32) * gamma[h:h + 1]).astype(jnp.bfloat16)
-
-
-def scale(hm, w, kw):
+        w_v[:, cols] = (w_v[:, cols].astype(jnp.float32) * gamma[h:h + 1]).astype(jnp.bfloat16)
+    stores[1].start()
+    loads[2].wait()
+    stores[2].start()
+    lane = lax.broadcasted_iota(jnp.int32, (1, 128), 1)
+    row = jnp.zeros((1, 128), jnp.float32)
+    for h in range(8):
+        row = jnp.where(lane == h, mine[h:h + 1, :], row)
+    top_ref[...] = row[:, :8]
+    for cp in stores:
+        cp.wait()
+
+
+def scale(hm, w, kw, att):
     vm = pl.BlockSpec(memory_space=pltpu.VMEM)
+    hbm = pl.BlockSpec(memory_space=pl.ANY)
+    full = jax.ShapeDtypeStruct(w.shape, w.dtype)
     return pl.pallas_call(
         scale_kernel,
-        out_shape=(jax.ShapeDtypeStruct(w.shape, w.dtype),
-                   jax.ShapeDtypeStruct(kw.shape, kw.dtype),
-                   jax.ShapeDtypeStruct((8, 128), jnp.float32)),
-        in_specs=[vm] * 3, out_specs=(vm,) * 3, name="scale",
-    )(hm, w, kw)
+        out_shape=(full, full, full, jax.ShapeDtypeStruct((1, 8), jnp.float32)),
+        in_specs=[vm, hbm, hbm, hbm], out_specs=(hbm, hbm, hbm, vm),
+        scratch_shapes=[pltpu.VMEM(w.shape, w.dtype)] * 3 + [pltpu.SemaphoreType.DMA((3,))] * 2,
+        compiler_params=pltpu.CompilerParams(vmem_limit_bytes=67043328),
+        name="scale",
+    )(hm, w, kw, att)
 
 
 def shards(q, k, v, w, kw):
     out, hm = attend_all(q, k, v)
-    w_out, k_out, top = scale(hm, w, kw)
-    return out, top[:, 0], w_out, k_out
+    w_out, k_out, att, top = scale(hm, w, kw, out)
+    return att, top.reshape(8), w_out, k_out
 
 
 def solution(mesh):

time: 72 us -> 69.8 us (0.969)
  local copies, waits for them, and re-layouts: 2.11 us -> 0 us
    unnamed x5 -> x0, local copies, waits for them, and re-layouts: 1.48 us -> none
    pallas_call x1, Pallas kernels: 66.7 us -> 65.3 us  [attend_all(): pl.pallas_call(attention_kernel, out_shape=(jax.ShapeDtypeStruct((ROWS, 1...]
    pallas_call x1, Pallas kernels: 2.46 us -> 3.73 us  [scale(): pl.pallas_call(scale_kernel, out_shape=(full, full, full, jax.ShapeDtypeS...]
where the time goes in v4:
time: 69.8 us; the launch traced here: 69.7 us
  Pallas kernels  69.1 us (99%)
    pallas_call x1, Pallas kernels, attend_all(): pl.pallas_call(attention_kernel, out_shape=(jax.ShapeDtypeStruct((ROWS, 1...  65.3 us
    pallas_call x1, Pallas kernels, scale(): pl.pallas_call(scale_kernel, out_shape=(full, full, full, jax.ShapeDtypeS...  3.73 us

profile of v4, /device:TPU:32, one launch (start us, length us, event | category | flops | bytes accessed | tf_op | source)
XLA Modules:
  0.0 69.7 jit_solution(5305916690891136872)
XLA Ops:
  0.6 65.3 %attend.1 = (bf16[256,1024]{1,0:T(8,128)(2,1)}, f32[128,128]{1,0:T(8,128)}) custom-call(bf16[256,1024]{1,0:T(8,128)(2,1)} %q_hbm.1, bf16[256,128]{1,0:T(8,128)(2,1)} %k_hbm.1, bf16[256,128]{1,0:T(8,128)(2,1)} %v_hbm.1), custom_call_target="tpu_custom_call" | custom-call | tf_op jit(solution)/shard_map/attend/pallas_call | solution.py:429
  66.0 3.7 %scale.1 = (bf16[256,1024]{1,0:T(8,128)(2,1)}, bf16[256,1024]{1,0:T(8,128)(2,1)}, bf16[256,1024]{1,0:T(8,128)(2,1)}, f32[1,8]{1,0:T(1,128)}) custom-call(f32[128,128]{1,0:T(8,128)} %get-tuple-element.10.hm_ref, bf16[256,1024]{1,0:T(8,128)(2,1)} %w_hbm.1, bf16[256,1024]{1,0:T(8,128)(2,1)} %kw_hbm.1, bf16[256,1024]{1,0:T(8,128)(2,1)} %get-tuple-element.11.att_hbm), custom_call_target="tpu_custom_call" | custom-call | tf_op jit(solution)/shard_map/scale/pallas_call | solution.py:507

commit v5 on v4

--- a/solution.py
+++ b/solution.py
@@ -12,7 +12,7 @@
 NZ, NX = 8, 4
 TAU = 10.0
 NEG = -1e30
-LATE = 3
+LATE = 2
 LEAD1, LEAD2 = 4, 2
 LOG2_SCALE = math.log2(math.e) / math.sqrt(128.0)
 MESH = pl.DeviceIdType.MESH
@@ -83,20 +83,21 @@
             src_ref=src, dst_ref=dst, send_sem=send, recv_sem=recv,
             device_id=dev, device_id_type=MESH)
 
-    def blk(row, col):
-        return kv.at[row, col]
-
-    def zcopy(row, slot, dev):
-        return remote(blk(row, x), blk(row, x), zs_sem.at[slot], kv_sem.at[row, x], (dev, t))
-
-    def xcopy(n, j, row, col, dev):
-        return remote(blk(row, col), blk(row, col), xs_sem.at[n, j], kv_sem.at[row, col], (dev, t))
-
-    def dcopy(row, col):
-        return remote(blk(row, col), blk(row, col), ds_sem.at[row, col], kv_sem.at[row, col], (s, sib))
-
-    def arrived(row, col):
-        pltpu.make_async_copy(blk(row, col), blk(row, col), kv_sem.at[row, col]).wait()
+    def zcopy(row, slot, dev, j):
+        b = kv.at[row, x, j]
+        return remote(b, b, zs_sem.at[slot, j], kv_sem.at[row, x, j], (dev, t))
+
+    def xcopy(n, way, row, col, dev, j):
+        b = kv.at[row, col, j]
+        return remote(b, b, xs_sem.at[n, way, j], kv_sem.at[row, col, j], (dev, t))
+
+    def dcopy(row, col, j):
+        b = kv.at[row, col, j]
+        return remote(b, b, ds_sem.at[row, col, j], kv_sem.at[row, col, j], (s, sib))
+
+    def arrived(row, col, j):
+        b = kv.at[row, col, j]
+        pltpu.make_async_copy(b, b, kv_sem.at[row, col, j]).wait()
 
     def order(n):
         nu = rh + 2
@@ -114,76 +115,82 @@
     xp1 = lax.rem(x + 1, NX)
     xp2 = lax.rem(x + 2, NX)
 
-    def fwd_copies(n):
-        row, from_u = order(n)
-        even = lax.rem(row, 2) == 0
-        return (even, xcopy(n, 2, row, xm1, xr), xcopy(n, 2, row, xp1, xl))
-
     def stage1(n, first):
         row, from_u = order(n)
 
         @pl.when(driver)
         def _():
-            if first:
-                @pl.when(pu < 5)
-                def _():
-                    zcopy(row, 0, zu).start()
-
-                @pl.when(pd < 5)
-                def _():
-                    zcopy(row, 8, zd).start()
-            else:
-                arrived(row, x)
-
-                @pl.when(jnp.logical_and(from_u, pu < 5))
-                def _():
-                    zcopy(row, n, zu).start()
-
-                @pl.when(jnp.logical_and(jnp.logical_not(from_u), pd < 5))
-                def _():
-                    zcopy(row, n, zd).start()
-            xcopy(n, 0, row, x, xr).start()
-            xcopy(n, 1, row, x, xl).start()
-            dcopy(row, x).start()
+            for j in range(2):
+                if first:
+                    @pl.when(pu < 5)
+                    def _():
+                        zcopy(row, 0, zu, j).start()
+
+                    @pl.when(pd < 5)
+                    def _():
+                        zcopy(row, 8, zd, j).start()
+                else:
+                    arrived(row, x, j)
+
+                    @pl.when(jnp.logical_and(from_u, pu < 5))
+                    def _():
+                        zcopy(row, n, zu, j).start()
+
+                    @pl.when(jnp.logical_and(jnp.logical_not(from_u), pd < 5))
+                    def _():
+                        zcopy(row, n, zd, j).start()
+                xcopy(n, 0, row, x, xr, j).start()
+                xcopy(n, 1, row, x, xl, j).start()
+                dcopy(row, x, j).start()
 
     def stage2(n):
         row, _ = order(n)
 
         @pl.when(driver)
         def _():
-            even, right, left = fwd_copies(n)
-            arrived(row, xm1)
-
-            @pl.when(even)
-            def _():
-                right.start()
-            dcopy(row, xm1).start()
-            arrived(row, xp1)
-
-            @pl.when(jnp.logical_not(even))
-            def _():
-                left.start()
-            dcopy(row, xp1).start()
+            even = lax.rem(row, 2) == 0
+            for j in range(2):
+                arrived(row, xm1, j)
+
+                @pl.when(even)
+                def _():
+                    xcopy(n, 2, row, xm1, xr, j).start()
+                dcopy(row, xm1, j).start()
+                arrived(row, xp1, j)
+
+                @pl.when(jnp.logical_not(even))
+                def _():
+                    xcopy(n, 2, row, xp1, xl, j).start()
+                dcopy(row, xp1, j).start()
 
     def stage3(n):
         row, _ = order(n)
 
         @pl.when(driver)
         def _():
-            arrived(row, xp2)
-            dcopy(row, xp2).start()
+            for j in range(2):
+                arrived(row, xp2, j)
+                dcopy(row, xp2, j).start()
 
         @pl.when(foreign)
         def _():
             for col in range(NX):
-                arrived(row, col)
-
-    own_down = remote(tr.at[0], kv.at[r, x], zs_sem.at[0], kv_sem.at[r, x], (zd, t))
-    own_up = remote(tr.at[0], kv.at[r, x], zs_sem.at[0], kv_sem.at[r, x], (zu, t))
-    hop_down = remote(tr.at[0], tr.at[1], zs_sem.at[0], tr_sem, (zd, t))
-    hop_up = remote(tr.at[0], tr.at[1], zs_sem.at[0], tr_sem, (zu, t))
-    fwd_down = remote(tr.at[1], kv.at[5, x], zs_sem.at[1], kv_sem.at[5, x], (zd, t))
-    fwd_up = remote(tr.at[1], kv.at[6, x], zs_sem.at[1], kv_sem.at[6, x], (zu, t))
+                for j in range(2):
+                    arrived(row, col, j)
+
+    def hop(src, dst, slot, recv, dev):
+        return [remote(src.at[j], dst.at[j], zs_sem.at[slot, j], recv.at[j], (dev, t))
+                for j in range(2)]
+
+    def land(row):
+        return kv.at[row, x], kv_sem.at[row, x]
+
+    own_down = hop(tr.at[0], land(r)[0], 0, land(r)[1], zd)
+    own_up = hop(tr.at[0], land(r)[0], 0, land(r)[1], zu)
+    hop_down = hop(tr.at[0], tr.at[1], 0, tr_sem, zd)
+    hop_up = hop(tr.at[0], tr.at[1], 0, tr_sem, zu)
+    fwd_down = hop(tr.at[1], land(5)[0], 1, land(5)[1], zd)
+    fwd_up = hop(tr.at[1], land(6)[0], 1, land(6)[1], zu)
 
     q_sib = remote(qv.at[1], qin.at[0], qs_sem.at[0], q_sem.at[0], (s, sib))
     q_par = remote(qv.at[0], qin.at[1], qs_sem.at[0], q_sem.at[1], (part, t))
@@ -199,10 +206,11 @@
     def _():
         tr_k.wait()
         tr_v.wait()
-        for rr, cp in ((4, own_down), (5, hop_down), (6, hop_up), (7, own_up)):
+        for rr, cps in ((4, own_down), (5, hop_down), (6, hop_up), (7, own_up)):
             @pl.when(r == rr)
             def _():
-                cp.start()
+                for cp in cps:
+                    cp.start()
 
     q_lo.wait()
     q_hi.wait()
@@ -213,11 +221,13 @@
 
     @pl.when(foreign)
     def _():
-        for rr, cp in ((4, fwd_down), (7, fwd_up)):
+        for rr, cps in ((4, fwd_down), (7, fwd_up)):
             @pl.when(r == rr)
             def _():
-                pltpu.make_async_copy(tr.at[1], tr.at[1], tr_sem).wait()
-                cp.start()
+                for j, cp in enumerate(cps):
+                    b = tr.at[1, j]
+                    pltpu.make_async_copy(b, b, tr_sem.at[j]).wait()
+                    cp.start()
         q_par.start()
         q_pas.start()
 
@@ -378,29 +388,30 @@
 
     @pl.when(driver)
     def _():
-        @pl.when(pu < 5)
-        def _():
-            zcopy(r, 0, zu).wait_send()
-
-        @pl.when(pd < 5)
-        def _():
-            zcopy(r, 8, zd).wait_send()
+        for j in range(2):
+            @pl.when(pu < 5)
+            def _():
+                zcopy(r, 0, zu, j).wait_send()
+
+            @pl.when(pd < 5)
+            def _():
+                zcopy(r, 8, zd, j).wait_send()
 
         def drain(n, carry):
             row, from_u = order(n)
-
-            @pl.when(jnp.logical_and(n > 0, jnp.logical_and(from_u, pu < 5)))
-            def _():
-                zcopy(row, n, zu).wait_send()
-
-            @pl.when(jnp.logical_and(n > 0, jnp.logical_and(jnp.logical_not(from_u), pd < 5)))
-            def _():
-                zcopy(row, n, zd).wait_send()
-            xcopy(n, 0, row, x, xr).wait_send()
-            xcopy(n, 1, row, x, xl).wait_send()
-            xcopy(n, 2, row, xm1, xr).wait_send()
-            for col in range(NX):
-                dcopy(row, col).wait_send()
+            for j in range(2):
+                @pl.when(jnp.logical_and(n > 0, jnp.logical_and(from_u, pu < 5)))
+                def _():
+                    zcopy(row, n, zu, j).wait_send()
+
+                @pl.when(jnp.logical_and(n > 0, jnp.logical_and(jnp.logical_not(from_u), pd < 5)))
+                def _():
+                    zcopy(row, n, zd, j).wait_send()
+                xcopy(n, 0, row, x, xr, j).wait_send()
+                xcopy(n, 1, row, x, xl, j).wait_send()
+                xcopy(n, 2, row, xm1, xr, j).wait_send()
+                for col in range(NX):
+                    dcopy(row, col, j).wait_send()
             return carry
 
         lax.fori_loop(0, NZ, drain, 0)
@@ -411,11 +422,13 @@
 
     @pl.when(foreign)
     def _():
-        own_down.wait_send()
+        for cp in own_down:
+            cp.wait_send()
 
         @pl.when(jnp.logical_or(r == 4, r == 7))
         def _():
-            fwd_down.wait_send()
+            for cp in fwd_down:
+                cp.wait_send()
         q_par.wait_send()
         q_pas.wait_send()
         back_s.wait_send()
@@ -443,13 +456,13 @@
             pltpu.VMEM((2, 4, ROWS, 128), jnp.float32),
             pltpu.VMEM((2, ROWS, 512), bf),
             pltpu.SemaphoreType.DMA((4,)),
-            pltpu.SemaphoreType.DMA((NZ, NX)),
-            pltpu.SemaphoreType.DMA,
+            pltpu.SemaphoreType.DMA((NZ, NX, 2)),
             pltpu.SemaphoreType.DMA((2,)),
             pltpu.SemaphoreType.DMA((2,)),
-            pltpu.SemaphoreType.DMA((9,)),
-            pltpu.SemaphoreType.DMA((NZ, 3)),
-            pltpu.SemaphoreType.DMA((NZ, NX)),
+            pltpu.SemaphoreType.DMA((2,)),
+            pltpu.SemaphoreType.DMA((9, 2)),
+            pltpu.SemaphoreType.DMA((NZ, 3, 2)),
+            pltpu.SemaphoreType.DMA((NZ, NX, 2)),
             pltpu.SemaphoreType.DMA((2,)),
             pltpu.SemaphoreType.DMA((2,)),
             pltpu.VMEM((3, 8, 128), jnp.float32),

time: 69.8 us -> 68.2 us (0.977)
  the two profiles are of different devices: /device:TPU:32 before, /device:TPU:192 now
where the time goes in v5:
time: 68.2 us; the launch traced here: 68 us
  Pallas kernels  67.4 us (99%)
    pallas_call x1, Pallas kernels, attend_all(): pl.pallas_call(attention_kernel, out_shape=(jax.ShapeDtypeStruct((ROWS, 1...  63.6 us
    pallas_call x1, Pallas kernels, scale(): pl.pallas_call(scale_kernel, out_shape=(full, full, full, jax.ShapeDtypeS...  3.73 us

profile of v5, /device:TPU:192, one launch (start us, length us, event | category | flops | bytes accessed | tf_op | source)
XLA Modules:
  0.0 68.0 jit_solution(14764893299782807417)
XLA Ops:
  0.6 63.6 %attend.1 = (bf16[256,1024]{1,0:T(8,128)(2,1)}, f32[128,128]{1,0:T(8,128)}) custom-call(bf16[256,1024]{1,0:T(8,128)(2,1)} %q_hbm.1, bf16[256,128]{1,0:T(8,128)(2,1)} %k_hbm.1, bf16[256,128]{1,0:T(8,128)(2,1)} %v_hbm.1), custom_call_target="tpu_custom_call" | custom-call | tf_op jit(solution)/shard_map/attend/pallas_call | solution.py:442
  64.3 3.7 %scale.1 = (bf16[256,1024]{1,0:T(8,128)(2,1)}, bf16[256,1024]{1,0:T(8,128)(2,1)}, bf16[256,1024]{1,0:T(8,128)(2,1)}, f32[1,8]{1,0:T(1,128)}) custom-call(f32[128,128]{1,0:T(8,128)} %get-tuple-element.10.hm_ref, bf16[256,1024]{1,0:T(8,128)(2,1)} %w_hbm.1, bf16[256,1024]{1,0:T(8,128)(2,1)} %kw_hbm.1, bf16[256,1024]{1,0:T(8,128)(2,1)} %get-tuple-element.11.att_hbm), custom_call_target="tpu_custom_call" | custom-call | tf_op jit(solution)/shard_map/scale/pallas_call | solution.py:520

commit v6 on v5

--- a/solution.py
+++ b/solution.py
@@ -13,7 +13,7 @@
 TAU = 10.0
 NEG = -1e30
 LATE = 2
-LEAD1, LEAD2 = 4, 2
+LEAD1, LEAD2 = 5, 3
 LOG2_SCALE = math.log2(math.e) / math.sqrt(128.0)
 MESH = pl.DeviceIdType.MESH
 

time: 68.2 us -> 68.8 us (level)
  the two profiles are of different devices: /device:TPU:192 before, /device:TPU:32 now
where the time goes in v6:
time: 68.8 us; the launch traced here: 68.6 us
  Pallas kernels  68 us (99%)
    pallas_call x1, Pallas kernels, attend_all(): pl.pallas_call(attention_kernel, out_shape=(jax.ShapeDtypeStruct((ROWS, 1...  64.2 us
    pallas_call x1, Pallas kernels, scale(): pl.pallas_call(scale_kernel, out_shape=(full, full, full, jax.ShapeDtypeS...  3.73 us

profile of v6, /device:TPU:32, one launch (start us, length us, event | category | flops | bytes accessed | tf_op | source)
XLA Modules:
  0.0 68.6 jit_solution(16865750425873547668)
XLA Ops:
  0.6 64.2 %attend.1 = (bf16[256,1024]{1,0:T(8,128)(2,1)}, f32[128,128]{1,0:T(8,128)}) custom-call(bf16[256,1024]{1,0:T(8,128)(2,1)} %q_hbm.1, bf16[256,128]{1,0:T(8,128)(2,1)} %k_hbm.1, bf16[256,128]{1,0:T(8,128)(2,1)} %v_hbm.1), custom_call_target="tpu_custom_call" | custom-call | tf_op jit(solution)/shard_map/attend/pallas_call | solution.py:442
  64.9 3.7 %scale.1 = (bf16[256,1024]{1,0:T(8,128)(2,1)}, bf16[256,1024]{1,0:T(8,128)(2,1)}, bf16[256,1024]{1,0:T(8,128)(2,1)}, f32[1,8]{1,0:T(1,128)}) custom-call(f32[128,128]{1,0:T(8,128)} %get-tuple-element.10.hm_ref, bf16[256,1024]{1,0:T(8,128)(2,1)} %w_hbm.1, bf16[256,1024]{1,0:T(8,128)(2,1)} %kw_hbm.1, bf16[256,1024]{1,0:T(8,128)(2,1)} %get-tuple-element.11.att_hbm), custom_call_target="tpu_custom_call" | custom-call | tf_op jit(solution)/shard_map/scale/pallas_call | solution.py:520
